TPU v7x, 32 devices: a whole 2x2x4 slice. The times are simulated.
32 devices in a mesh: pw: 2 (over x), pair: 16 (over z, y, core).
Axes of the slice: x: 2, y: 2, z: 4, core: 2. Of those that a mesh axis runs over, the one named last changes fastest.
Arguments:
- valence_pairs: bfloat16 [64, 64, 8192], P('pair', None, 'pw'), may hold values from -0.59765625 to 0.59765625
- conduction_pairs: bfloat16 [16, 256, 8192], P('pair', None, 'pw'), may hold values from -0.59765625 to 0.59765625
- screening: float32 [8192], P('pw'), may hold values from 0.1 to 2
Outputs:
- kernel: float32 [64, 16, 64, 256], P('pair', None, 'pw')
All inputs are finite; a program needn't handle non-finite values.
Results may differ from a plain program's by a relative error of at most 0.0029.
Values may be sent and summed in bfloat16 or wider, within the bound.
A program may use at most 128 MiB of HBM per device.

v0:
```python
import jax
import jax.numpy as jnp
from jax import lax
from jax.sharding import PartitionSpec as P


def contract(piece, flat_right, band_dev, conduction):
    first, second, width = piece.shape
    product = lax.dot_general(
        piece.reshape(first * second, width),
        flat_right,
        (((1,), (1,)), ((), ())),
        preferred_element_type=jnp.float32,
    )
    return product.reshape(first, second, band_dev, conduction)


def route_rows(terms):
    owned = lax.all_to_all(terms, "pair", split_axis=0, concat_axis=2, tiled=True)
    return owned.transpose(0, 2, 1, 3)


def body(valence_pairs, conduction_pairs, screening):
    screened = (valence_pairs.astype(jnp.float32) * screening[None, None, :]).astype(jnp.bfloat16)
    band_dev, conduction, plane_dev = conduction_pairs.shape
    flat_local = conduction_pairs.reshape(band_dev * conduction, plane_dev)
    partial_value = contract(
        lax.all_gather(screened, "pair", axis=0, tiled=True), flat_local, band_dev, conduction
    )
    terms = lax.psum_scatter(partial_value, "pw", scatter_dimension=1, tiled=True)
    return route_rows(terms)


def solution(mesh):
    placed = (P("pair", None, "pw"), P("pair", None, "pw"), P("pw"))
    return jax.shard_map(
        body, mesh=mesh, in_specs=placed, out_specs=P("pair", None, "pw", None), check_vma=False
    )
```

profile of v0, /device:TPU:1, one launch (start us, length us, event | category | flops | bytes accessed | tf_op | source)
XLA Modules:
  0.0 314.3 jit_solution(8804609150901646009)
XLA Ops:
  6.5 0.0 copy-start
  6.5 0.0 all-gather.2.cloned.1.call-start
  6.5 3.5 %multiply_convert_fusion = bf16[4,64,4096]{2,1,0:T(8,128)(2,1)} fusion(bf16[4,64,4096]{2,1,0:T(8,128)(2,1)} %param.3, f32[4096]{0:T(1024)} %param.5), kind=kLoop, calls=%fused_computation | loop fusion | flops 3145728 | bytes 4210688 | tf_op jit(solution)/shard_map/convert_element_type | solution.py:24
  10.1 0.0 all-gather.2.cloned.1.call-update
  10.1 0.0 reduce-scatter.2.cloned.1.call-start
  10.1 170.6 %all-gather.2.cloned.1.call-done = bf16[64,64,4096]{2,1,0:T(8,128)(2,1)} async-done(((bf16[4,64,4096]{2,1,0:T(8,128)(2,1)}), bf16[64,64,4096]{2,1,0:T(8,128)(2,1)}) %all-gather.2.cloned.1.call-update) | async-done | bytes 33554448 | tf_op jit(solution)/shard_map/all_gather | solution.py:28
  180.8 0.0 copy-done
  180.8 17.2 %convolution_bitcast_fusion = f32[64,64,1,256]{3,1,0,2:T(8,128)} fusion(bf16[64,64,4096]{2,1,0:T(8,128)(2,1)} %all-gather.2.cloned.1.call-done, bf16[1,256,4096]{2,1,0:T(8,128)(2,1)S(1)} %copy-done), kind=kOutput, calls=%fused_computation.1 | convolution fusion | flops 8589934592 | bytes 39845888 | tf_op jit(solution)/shard_map/dot_general | solution.py:9
  198.0 0.0 reduce-scatter.2.cloned.1.call-update
  198.0 53.9 %reduce-scatter.2.cloned.1.call-done = f32[64,32,1,256]{3,1,0,2:T(8,128)} async-done(((f32[64,64,1,256]{3,1,0,2:T(8,128)}), f32[64,32,1,256]{3,1,0,2:T(8,128)}) %reduce-scatter.2.cloned.1.call-update) | async-done | bytes 2097168 | tf_op jit(solution)/shard_map/reduce_scatter | solution.py:30
  251.9 54.1 %all_to_all.18 = f32[64,32,1,256]{3,1,2,0:T(8,128)S(1)} all-to-all(f32[64,32,1,256]{3,1,2,0:T(8,128)} %bitcast.17), channel_id=1, replica_groups=mesh['pw'=2,'pair'=16] {'pair'}, dimensions={0} | all-to-all | bytes 4194304 | tf_op jit(solution)/shard_map/all_to_all | solution.py:19
  306.0 1.5 copy.8
Async XLA Ops:
  6.5 174.2 %copy-start = (bf16[1,256,4096]{2,1,0:T(8,128)(2,1)S(1)}, bf16[1,256,4096]{2,1,0:T(8,128)(2,1)}, u32[]{:S(2)}) copy-start(bf16[1,256,4096]{2,1,0:T(8,128)(2,1)} %param.4) | copy-start | bytes 6291460
  6.5 174.2 %all-gather.2.cloned.1.call-start = ((), (), s32[]{:S(2)}) async-start(), calls=%async_computation.2 | async-start | bytes 35651584 | tf_op jit(solution)/shard_map/all_gather | solution.py:28
  10.1 241.8 %reduce-scatter.2.cloned.1.call-start = ((), (), s32[]{:S(2)}) async-start(), calls=%async_computation.3 | async-start | bytes 6291456 | tf_op jit(solution)/shard_map/reduce_scatter | solution.py:30
Sparse Core Ops, SparseCore 0:
  10.2 170.5 all-gather.1
  198.1 53.7 reduce-scatter.1
where the time goes:
time: 314 us
  waiting for transfers between devices  225 us (72%)
  blocking collectives  54.1 us (17%)
  matrix products  17.2 us (5%)
  between operations  13.4 us (4%)
  other arithmetic  3.53 us (1%)
    all_gather x1, waiting for transfers between devices, body(): lax.all_gather(screened, 'pair', axis=0, tiled=True)  171 us
    all_to_all x1, blocking collectives, route_rows(): lax.all_to_all(terms, 'pair', split_axis=0, concat_axis=2, tiled=True)  54.1 us
    reduce_scatter x1, waiting for transfers between devices, body(): lax.psum_scatter(partial_value, 'pw', scatter_dimension=1, tiled=True)  53.9 us
    dot_general x1, matrix products, contract(): lax.dot_general(piece.reshape(first * second, width), flat_right, (((1,),...  17.2 us
  transfers between devices with their start and end apart: 2, of which 2 were waited for; matrix products, arithmetic and copies ran while one was open for 0% of the time, Pallas kernels for 0%

commit v1 on v0

--- a/solution.py
+++ b/solution.py
@@ -16,7 +16,9 @@
 
 
 def route_rows(terms):
-    owned = lax.all_to_all(terms, "pair", split_axis=0, concat_axis=2, tiled=True)
+    owned = jnp.concatenate(
+        lax.all_to_all(jnp.stack(jnp.split(terms, lax.psum(1, "pair"), 0)), "pair", 0, 0), 2
+    )
     return owned.transpose(0, 2, 1, 3)
 
 

time: 314 us -> 329 us (1.048)
  local copies, waits for them, and re-layouts: 1.46 us -> 16.1 us
    unnamed x2 -> x17, local copies, waits for them, and re-layouts: 0.01 us -> 13.7 us
where the time goes in v1:
time: 329 us
  waiting for transfers between devices  225 us (68%)
  blocking collectives  53.9 us (16%)
  matrix products  17.2 us (5%)
  local copies, waits for them, and re-layouts  16.1 us (5%)
  between operations  13.5 us (4%)
  other arithmetic  3.53 us (1%)
    all_gather x1, waiting for transfers between devices, body(): lax.all_gather(screened, 'pair', axis=0, tiled=True)  171 us
    reduce_scatter x1, waiting for transfers between devices, body(): lax.psum_scatter(partial_value, 'pw', scatter_dimension=1, tiled=True)  53.9 us
    all_to_all x1, blocking collectives, route_rows(): lax.all_to_all(jnp.stack(jnp.split(terms, lax.psum(1, 'pair'), 0)), 'pair...  53.9 us
    dot_general x1, matrix products, contract(): lax.dot_general(piece.reshape(first * second, width), flat_right, (((1,),...  17.2 us
    unnamed x17, local copies, waits for them, and re-layouts  13.7 us
  transfers between devices with their start and end apart: 2, of which 2 were waited for; matrix products, arithmetic and copies ran while one was open for 0% of the time, Pallas kernels for 0%

profile of v1, /device:TPU:1, one launch (start us, length us, event | category | flops | bytes accessed | tf_op | source)
XLA Modules:
  0.0 328.8 jit_solution(3767684782937142935)
XLA Ops:
  6.5 0.0 copy-start
  6.5 0.0 all-gather.2.cloned.1.call-start
  6.5 3.5 %multiply_convert_fusion = bf16[4,64,4096]{2,1,0:T(8,128)(2,1)} fusion(bf16[4,64,4096]{2,1,0:T(8,128)(2,1)} %param.3, f32[4096]{0:T(1024)} %param.5), kind=kLoop, calls=%fused_computation | loop fusion | flops 3145728 | bytes 4210688 | tf_op jit(solution)/shard_map/convert_element_type | solution.py:26
  10.1 0.0 all-gather.2.cloned.1.call-update
  10.1 0.0 reduce-scatter.2.cloned.1.call-start
  10.1 170.6 %all-gather.2.cloned.1.call-done = bf16[64,64,4096]{2,1,0:T(8,128)(2,1)} async-done(((bf16[4,64,4096]{2,1,0:T(8,128)(2,1)}), bf16[64,64,4096]{2,1,0:T(8,128)(2,1)}) %all-gather.2.cloned.1.call-update) | async-done | bytes 33554448 | tf_op jit(solution)/shard_map/all_gather | solution.py:30
  180.8 0.0 copy-done
  180.8 17.2 %convolution_bitcast_fusion = f32[64,64,1,256]{3,1,0,2:T(8,128)} fusion(bf16[64,64,4096]{2,1,0:T(8,128)(2,1)} %all-gather.2.cloned.1.call-done, bf16[1,256,4096]{2,1,0:T(8,128)(2,1)S(1)} %copy-done), kind=kOutput, calls=%fused_computation.1 | convolution fusion | flops 8589934592 | bytes 39845888 | tf_op jit(solution)/shard_map/dot_general | solution.py:9
  198.0 0.0 reduce-scatter.2.cloned.1.call-update
  198.0 53.9 %reduce-scatter.2.cloned.1.call-done = f32[64,32,1,256]{3,1,0,2:T(8,128)} async-done(((f32[64,64,1,256]{3,1,0,2:T(8,128)}), f32[64,32,1,256]{3,1,0,2:T(8,128)}) %reduce-scatter.2.cloned.1.call-update) | async-done | bytes 2097168 | tf_op jit(solution)/shard_map/reduce_scatter | solution.py:32
  251.9 0.9 fusion.16
  252.8 0.9 fusion.15
  253.8 0.9 fusion.14
  254.7 0.9 fusion.13
  255.6 0.9 fusion.12
  256.5 0.9 fusion.11
  257.4 0.9 fusion.10
  258.4 0.9 fusion.9
  259.3 0.9 fusion.8
  260.2 0.9 fusion.7
  261.1 0.9 fusion.6
  262.0 0.9 fusion.5
  263.0 0.9 fusion.4
  263.9 0.9 fusion.3
  264.8 0.9 fusion.2
  265.7 0.9 fusion.1
  266.6 53.9 %all_to_all.5 = f32[16,4,32,1,256]{4,2,1,3,0:T(8,128)S(1)} all-to-all(f32[16,4,32,1,256]{4,2,1,3,0:T(8,128)S(1)} %fusion.1), channel_id=1, replica_groups=mesh['pw'=2,'pair'=16] {'pair'}, dimensions={0} | all-to-all | bytes 4194304 | tf_op jit(solution)/shard_map/all_to_all | solution.py:20
  320.5 1.5 copy.5
Async XLA Ops:
  6.5 174.2 %copy-start = (bf16[1,256,4096]{2,1,0:T(8,128)(2,1)S(1)}, bf16[1,256,4096]{2,1,0:T(8,128)(2,1)}, u32[]{:S(2)}) copy-start(bf16[1,256,4096]{2,1,0:T(8,128)(2,1)} %param.4) | copy-start | bytes 6291460
  6.5 174.2 %all-gather.2.cloned.1.call-start = ((), (), s32[]{:S(2)}) async-start(), calls=%async_computation.2 | async-start | bytes 35651584 | tf_op jit(solution)/shard_map/all_gather | solution.py:30
  10.1 241.8 %reduce-scatter.2.cloned.1.call-start = ((), (), s32[]{:S(2)}) async-start(), calls=%async_computation.3 | async-start | bytes 6291456 | tf_op jit(solution)/shard_map/reduce_scatter | solution.py:32
Sparse Core Ops, SparseCore 0:
  10.2 170.5 all-gather.1
  198.1 53.7 reduce-scatter.1
